TPU v7x, 32 devices: a whole 2x2x4 slice. The times are simulated.
32 devices in a mesh: seq: 8 (over z, y), tp: 4 (over x, core).
Axes of the slice: x: 2, y: 2, z: 4, core: 2. Of those that a mesh axis runs over, the one named last changes fastest.
Arguments:
- latents: bfloat16 [1024, 3072], P('seq', 'tp'), may hold values from -6 to 6
- lengths: int32 [2], replicated, may hold values from 1 to 768, 1024 in all
- t_index: int32 [2], replicated, may hold values from 0 to 6
- mod_scale: float32 [3072], replicated, may hold values from -2 to 2
- q_weight: bfloat16 [3072, 2048], P(None, 'tp'), may hold values from -0.109375 to 0.109375
- k_weight: bfloat16 [3072, 2048], P(None, 'tp'), may hold values from -0.109375 to 0.109375
- v_weight: bfloat16 [3072, 2048], P(None, 'tp'), may hold values from -0.109375 to 0.109375
- out_weight: bfloat16 [2048, 3072], P('tp'), may hold values from -0.1875 to 0.1875
- q_gain: float32 [128], replicated, may hold values from 0.6 to 2.4
- k_gain: float32 [128], replicated, may hold values from 0.6 to 2.4
- student_weight: bfloat16 [3072, 3072], P('tp'), may hold values from -0.15625 to 0.15625
Outputs:
- target: bfloat16 [1024, 3072], P('seq', 'tp')
- student_velocity: bfloat16 [1024, 3072], P('seq', 'tp')
- loss: float32 [], replicated
Inputs may be any that keep to these rules, and one draw needn't show every extreme that they name: lengths sum to 1024.
All inputs are finite; a program needn't handle non-finite values.
Results may differ from a plain program's by a relative error of at most 0.024.
Values may be sent and summed in bfloat16 or wider, within the bound.
No kernel may reach another device: no remote copies, remote signals or barrier semaphores. Data moves between devices by JAX's collectives and lax.ppermute only.
A program may use at most 64 MiB of HBM per device.

v0:
```python
import math
import jax
import jax.numpy as jnp
from jax import lax
from jax.sharding import PartitionSpec as P

TGRID = 8
epsilon = 1e-06
kinetic_weight = 0.1


def image_index(positions, image_ends):
    return jnp.sum((positions[:, None] >= image_ends[None, :]).astype(jnp.int32), axis=1)


def head_norm(projected, gain):
    shaped = projected.reshape(projected.shape[0], -1, gain.shape[0])
    normed = shaped * lax.rsqrt(jnp.mean(shaped * shaped, axis=-1, keepdims=True) + epsilon) * gain
    return normed.astype(jnp.bfloat16)


def teacher(
    state, times, query_image, image_ends, mod_scale, q_weight, k_weight, v_weight, q_gain, k_gain
):
    row_count = state.shape[0]
    head_dim = q_gain.shape[0]
    state32 = state.astype(jnp.float32)
    normed = state32 * lax.rsqrt(jnp.mean(state32 * state32, axis=1, keepdims=True) + epsilon)
    hidden = (normed * (1.0 + times[:, None] * mod_scale[None, :])).astype(jnp.bfloat16)
    queries = head_norm(jnp.dot(hidden, q_weight, preferred_element_type=jnp.float32), q_gain)
    key_rows = head_norm(jnp.dot(hidden, k_weight, preferred_element_type=jnp.float32), k_gain)
    key_rows = key_rows.reshape(row_count, -1)
    value_rows = jnp.dot(hidden, v_weight, preferred_element_type=jnp.float32).astype(jnp.bfloat16)
    heads_here = queries.shape[1]
    score_scale = 1.0 / math.sqrt(head_dim)

    def attend(carry, key_block, value_block):
        running_max, running_total, running_sum = carry
        count = key_block.shape[0]
        key_image = image_index(jnp.arange(count, dtype=jnp.int32), image_ends)
        key_heads = key_block.reshape(count, heads_here, head_dim)
        value_heads = value_block.reshape(count, heads_here, head_dim)
        same_image = (query_image[:, None] == key_image[None, :])[:, None, :]
        scores = (
            jnp.einsum("qhd,khd->qhk", queries, key_heads, preferred_element_type=jnp.float32)
            * score_scale
        )
        scores = jnp.where(same_image, scores, -1e30)
        new_max = jnp.maximum(running_max, jnp.max(scores, axis=2))
        weights = jnp.where(same_image, jnp.exp(scores - new_max[:, :, None]), 0.0)
        new_total = jnp.sum(weights, axis=2)
        product = jnp.einsum(
            "qhk,khd->qhd",
            weights.astype(jnp.bfloat16),
            value_heads,
            preferred_element_type=jnp.float32,
        )
        return (new_max, new_total, product)

    start_carry = (
        jnp.full((row_count, heads_here), -1e30, jnp.float32),
        jnp.zeros((row_count, heads_here), jnp.float32),
        jnp.zeros((row_count, heads_here, head_dim), jnp.float32),
    )
    offset = jnp.int32(0)
    key_block = lax.all_gather(key_rows, "seq", axis=0, tiled=True)
    value_block = lax.all_gather(value_rows, "seq", axis=0, tiled=True)
    count = key_block.shape[0]
    first_image = image_index(jnp.reshape(offset, (1,)), image_ends)[0]
    last_image = image_index(jnp.reshape(offset + count - 1, (1,)), image_ends)[0]
    touches = jnp.logical_and(first_image <= query_image[-1], last_image >= query_image[0])
    final_max, final_total, final_sum = lax.cond(
        touches,
        lambda inner: attend(inner, key_block, value_block),
        lambda inner: inner,
        start_carry,
    )
    mixed = (final_sum / final_total[:, :, None]).astype(jnp.bfloat16).reshape(row_count, -1)
    return (mixed, hidden)


def on_device(
    latents,
    lengths,
    t_index,
    mod_scale,
    q_weight,
    k_weight,
    v_weight,
    out_weight,
    q_gain,
    k_gain,
    student_weight,
):
    row_count, width_here = latents.shape
    tp_index = lax.axis_index("tp")
    image_ends = jnp.cumsum(lengths)
    row_offset = lax.axis_index("seq") * row_count
    query_image = image_index(row_offset + jnp.arange(row_count, dtype=jnp.int32), image_ends)
    one_hot = (
        query_image[:, None] == jnp.arange(lengths.shape[0], dtype=jnp.int32)[None, :]
    ).astype(jnp.float32)
    start_times = jnp.sum(one_hot * (t_index.astype(jnp.float32) / TGRID)[None, :], axis=1)
    step_size = 1.0 / TGRID
    whole_rows = lax.all_gather(latents, "tp", axis=1, tiled=True)
    velocities = []
    first_hidden = whole_rows
    state_shard = latents
    for euler_index in range(2):
        if euler_index == 1:
            whole_rows = lax.all_gather(state_shard, "tp", axis=1, tiled=True)
        mixed, hidden = teacher(
            whole_rows,
            start_times + euler_index * step_size,
            query_image,
            image_ends,
            mod_scale,
            q_weight,
            k_weight,
            v_weight,
            q_gain,
            k_gain,
        )
        if euler_index == 0:
            first_hidden = hidden
        partial_value = jnp.dot(mixed, out_weight, preferred_element_type=jnp.float32)
        velocity = lax.psum_scatter(
            partial_value.astype(jnp.bfloat16), "tp", scatter_dimension=1, tiled=True
        )
        velocities.append(velocity)
        state_shard = (
            latents.astype(jnp.float32) + step_size * velocity.astype(jnp.float32)
        ).astype(jnp.bfloat16)
    columns = lax.dynamic_slice_in_dim(first_hidden, tp_index * width_here, width_here, 1)
    student_terms = jnp.dot(columns, student_weight, preferred_element_type=jnp.float32)
    student_velocity = lax.psum_scatter(
        student_terms.astype(jnp.bfloat16), "tp", scatter_dimension=1, tiled=True
    )
    target = (0.5 * (velocities[0].astype(jnp.float32) + velocities[1].astype(jnp.float32))).astype(
        jnp.bfloat16
    )
    student32 = student_velocity.astype(jnp.float32)
    residual = student32 - target.astype(jnp.float32)
    per_token = jnp.sum(residual * residual, axis=1) + kinetic_weight * jnp.sum(
        student32 * student32, axis=1
    )
    image_part = jnp.sum(one_hot * per_token[:, None], axis=0)
    image_sum = lax.psum(image_part, ("seq", "tp"))
    loss = jnp.mean(image_sum / (lengths.astype(jnp.float32) * mod_scale.shape[0]))
    return (target, student_velocity, loss)


def solution(mesh):
    placed = (
        P("seq", "tp"),
        P(),
        P(),
        P(),
        P(None, "tp"),
        P(None, "tp"),
        P(None, "tp"),
        P("tp", None),
        P(),
        P(),
        P("tp", None),
    )
    return jax.shard_map(
        on_device,
        mesh=mesh,
        in_specs=placed,
        out_specs=(P("seq", "tp"), P("seq", "tp"), P()),
        check_vma=False,
    )
```

profile of v0, /device:TPU:0, one launch (start us, length us, event | category | flops | bytes accessed | tf_op | source)
XLA Modules:
  0.0 336.3 jit_solution(12734759485271382639)
XLA Ops:
  7.2 0.8 convert_multiply_fusion.6
  8.1 10.4 %all_gather.18 = bf16[128,3072]{1,0:T(8,128)(2,1)S(1)} all-gather(bf16[128,768]{1,0:T(8,128)(2,1)} %param.15), channel_id=1, replica_groups=mesh['seq'=8,'tp'=4] {'tp'}, dimensions={1}, use_global_device_ids=true | all-gather | bytes 983040 | tf_op jit(solution)/shard_map/all_gather | solution.py:105
  18.5 0.9 copy-done.2
  19.3 0.2 fusion.36
  19.6 0.8 reduce-window.4
  20.4 0.1 fusion.58
  20.5 0.1 select_reduce_fusion.1
  20.6 0.6 copy-done.10
  21.2 1.5 fusion.38
  22.7 0.9 copy-done.1
  23.6 3.1 convolution_convert_fusion.4
  26.8 3.4 %fusion.70 = (f32[128,512]{1,0:T(8,128)}, f32[128,512]{1,0:T(8,128)S(1)}) fusion(bf16[128,3072]{1,0:T(8,128)(2,1)} %copy-done.1, bf16[3072,512]{1,0:T(8,128)(2,1)} %param.20), kind=kOutput, calls=%fused_computation.115 | convolution fusion | flops 402718720 | bytes 4456448 | tf_op jit(solution)/shard_map/dot_general | solution.py:31
  30.2 1.8 mul.218
  32.0 1.2 reduce_sum.175
  33.2 0.2 mul.219
  33.4 0.7 fusion.52
  34.2 0.7 fusion.69
  34.8 0.6 fusion.60
  38.0 2.7 fusion.72
  40.7 0.8 reshape.212
  41.5 1.2 multiply_reduce_fusion.1
  42.8 0.1 fusion.56
  42.9 25.1 %all-gather.7.cloned.1.call-done = bf16[1024,512]{1,0:T(8,128)(2,1)} async-done(((bf16[128,512]{1,0:T(8,128)(2,1)}), bf16[1024,512]{1,0:T(8,128)(2,1)}) %all-gather.7.cloned.1.call-update) | async-done | bytes 1048592 | tf_op jit(solution)/shard_map/all_gather | solution.py:67
  68.0 41.7 %all-gather.5.cloned.1.call-done = bf16[1024,512]{1,0:T(8,128)(2,1)} async-done(((bf16[128,512]{1,0:T(8,128)(2,1)}), bf16[1024,512]{1,0:T(8,128)(2,1)}) %all-gather.5.cloned.1.call-update) | async-done | bytes 1048592 | tf_op jit(solution)/shard_map/all_gather | solution.py:66
  109.7 6.0 %conditional.2 = (f32[128,4]{0,1:T(4,128)S(1)}, f32[128,4,128]{0,2,1:T(8,128)S(1)}) conditional(s32[]{:T(128)} %convert_element_type.124, () %tuple.24, (s32[128]{0:T(128)S(1)}, s32[2]{0:T(128)}, bf16[1024,512]{1,0:T(8,128)(2,1)}, bf16[128,4,128]{2,0,1:T(8,128)(2,1)S(1)}, bf16[1024,512]{1,0:T(8,128)(2,1)}) %tuple.59), branch_computations={%region_8.9_spmd, %region_9.13_spmd} | conditional | flops 275386880 | bytes 14045748 | solution.py:72
  109.7 0.8 fusion.14
  110.5 0.2 broadcast_compare_fusion
  110.7 1.7 fusion
  112.5 1.6 convolution_bitcast_fusion
  114.1 0.5 fusion.2
  114.6 1.1 copy.83
  115.8 1.5 convolution_convert_fusion.1
  117.4 22.0 %reduce-scatter.4.cloned.1.call-done = bf16[128,768]{1,0:T(8,128)(2,1)} async-done(((bf16[128,3072]{1,0:T(8,128)(2,1)}), bf16[128,768]{1,0:T(8,128)(2,1)}) %reduce-scatter.4.cloned.1.call-update) | async-done | bytes 196624 | tf_op jit(solution)/shard_map/reduce_scatter | solution.py:127
  139.4 1.0 fusion.43
  140.4 8.0 %all_gather.21 = bf16[128,3072]{1,0:T(8,128)(2,1)S(1)} all-gather(bf16[128,768]{1,0:T(8,128)(2,1)S(1)} %fusion.43), channel_id=1, replica_groups=mesh['seq'=8,'tp'=4] {'tp'}, dimensions={1}, use_global_device_ids=true | all-gather | bytes 983040 | tf_op jit(solution)/shard_map/all_gather | solution.py:111
  148.4 0.2 fusion.39
  148.7 0.6 copy-done.3
  149.3 3.2 convolution_convert_fusion.3
  152.6 3.6 %fusion.71 = (f32[128,512]{1,0:T(8,128)}, f32[128,512]{1,0:T(8,128)}) fusion(bf16[3072,512]{1,0:T(8,128)(2,1)} %param.20, bf16[128,3072]{1,0:T(8,128)(2,1)} %copy-done.3, f32[128]{0:T(128)S(1)} %broadcast_add_fusion, f32[128]{0:T(128)S(1)} %add_rsqrt_fusion.4, f32[3072]{0:T(1024)S(1)} %copy-done.6), kind=kOutput, calls=%fused_computation.116 | convolution fusion | flops 405078016 | bytes 4469760 | tf_op jit(solution)/shard_map/dot_general | solution.py:31
  156.2 1.0 mul.240
  157.2 0.2 reduce_sum.178
  157.4 0.2 mul.241
  157.6 1.6 fusion.50
  159.4 4.2 %convolution_convert_fusion.2 = bf16[128,3072]{1,0:T(8,128)(2,1)} fusion(bf16[768,3072]{1,0:T(8,128)(2,1)} %param.25, bf16[128,3072]{1,0:T(8,128)(2,1)} %copy-done.1, s32[]{:T(128)S(6)} %select_n.16), kind=kOutput, calls=%fused_computation.48 | convolution fusion | flops 604372992 | bytes 5701636 | tf_op jit(solution)/shard_map/dot_general | solution.py:135
  163.7 3.5 %fusion.64 = f32[128,512]{1,0:T(8,128)} fusion(bf16[3072,512]{1,0:T(8,128)(2,1)} %param.19, bf16[128,3072]{1,0:T(8,128)(2,1)} %copy-done.3, f32[128]{0:T(128)S(1)} %broadcast_add_fusion, f32[128]{0:T(128)S(1)} %add_rsqrt_fusion.4, f32[3072]{0:T(1024)S(1)} %copy-done.6), kind=kOutput, calls=%fused_computation.112 | convolution fusion | flops 405012480 | bytes 4207616 | tf_op jit(solution)/shard_map/dot_general | solution.py:30
  167.2 1.0 reshape.214
  168.2 0.2 multiply_reduce_fusion
  168.5 1.1 fusion.54
  169.6 23.9 %all-gather.11.cloned.1.call-done = bf16[1024,512]{1,0:T(8,128)(2,1)} async-done(((bf16[128,512]{1,0:T(8,128)(2,1)}), bf16[1024,512]{1,0:T(8,128)(2,1)}) %all-gather.11.cloned.1.call-update) | async-done | bytes 1048592 | tf_op jit(solution)/shard_map/all_gather | solution.py:67
  193.5 41.6 %all-gather.9.cloned.1.call-done = bf16[1024,512]{1,0:T(8,128)(2,1)} async-done(((bf16[128,512]{1,0:T(8,128)(2,1)}), bf16[1024,512]{1,0:T(8,128)(2,1)}) %all-gather.9.cloned.1.call-update) | async-done | bytes 1048592 | tf_op jit(solution)/shard_map/all_gather | solution.py:66
  235.1 5.3 %conditional.3 = (f32[128,4]{0,1:T(4,128)S(1)}, f32[128,4,128]{0,2,1:T(8,128)S(1)}) conditional(s32[]{:T(128)} %convert_element_type.124, () %tuple.26, (s32[128]{0:T(128)S(1)}, s32[2]{0:T(128)S(1)}, bf16[1024,512]{1,0:T(8,128)(2,1)}, bf16[128,4,128]{2,0,1:T(8,128)(2,1)S(1)}, bf16[1024,512]{1,0:T(8,128)(2,1)}) %tuple.60), branch_computations={%region_17.18_spmd, %region_18.0_spmd} | conditional | flops 275386880 | bytes 14045748 | solution.py:72
  235.1 0.1 fusion.32
  235.2 0.2 broadcast_compare_fusion.1
  235.4 1.8 fusion.18
  237.2 1.6 convolution_bitcast_fusion.1
  238.8 0.5 fusion.20
  239.3 1.1 copy.85
  240.4 1.5 convolution_convert_fusion
  242.0 18.1 %reduce-scatter.8.cloned.1.call-done = bf16[128,768]{1,0:T(8,128)(2,1)} async-done(((bf16[128,3072]{1,0:T(8,128)(2,1)}), bf16[128,768]{1,0:T(8,128)(2,1)}) %reduce-scatter.8.cloned.1.call-update) | async-done | bytes 196624 | tf_op jit(solution)/shard_map/reduce_scatter | solution.py:136
  260.0 25.8 %reduce-scatter.6.cloned.1.call-done = bf16[128,768]{1,0:T(8,128)(2,1)} async-done(((bf16[128,3072]{1,0:T(8,128)(2,1)}), bf16[128,768]{1,0:T(8,128)(2,1)}) %reduce-scatter.6.cloned.1.call-update) | async-done | bytes 196624 | tf_op jit(solution)/shard_map/reduce_scatter | solution.py:127
  285.8 1.8 fusion.48
  287.6 0.1 select_reduce_fusion
  287.8 39.3 %psum.7 = f32[2]{0:T(128)S(1)} all-reduce(f32[2]{0:T(128)S(1)} %select_reduce_fusion), channel_id=1, replica_groups=mesh['seq'=8,'tp'=4] {'seq','tp'}, use_global_device_ids=true, to_apply=%region_27.28 | all-reduce | flops 2 | bytes 16 | tf_op jit(solution)/shard_map/psum | solution.py:148
  327.1 0.6 fusion.61
  (58 shorter events, 0.7 us)
Async XLA Ops:
  7.2 108.6 %copy-start = (bf16[512,3072]{1,0:T(8,128)(2,1)S(1)}, bf16[512,3072]{1,0:T(8,128)(2,1)}, u32[]{:S(2)}) copy-start(bf16[512,3072]{1,0:T(8,128)(2,1)} %param.22) | copy-start | bytes 9437188
  7.2 60.8 %all-gather.7.cloned.1.call-start = ((), (), s32[]{:S(2)}) async-start(), calls=%async_computation.4 | async-start | bytes 1179648 | tf_op jit(solution)/shard_map/all_gather | solution.py:67
  18.5 0.9 copy-start.2
  20.4 14.4 %copy-start.8 = (s32[2,1]{0,1:T(1,128)}, s32[2,1]{0,1:T(1,128)S(1)}, u32[]{:S(2)}) copy-start(s32[2,1]{0,1:T(1,128)S(1)} %reduce-window.4) | copy-start | bytes 28
  20.6 0.6 copy-start.10
  22.7 0.9 copy-start.1
  26.7 6.4 %copy-start.12 = (f32[128]{0:T(128)S(1)}, f32[128]{0:T(128)}, u32[]{:S(2)}) copy-start(f32[128]{0:T(128)} %param.24) | copy-start | bytes 1540
  26.7 83.0 %all-gather.5.cloned.1.call-start = ((), (), s32[]{:S(2)}) async-start(), calls=%async_computation.3 | async-start | bytes 1179648 | tf_op jit(solution)/shard_map/all_gather | solution.py:66
  34.1 105.3 %reduce-scatter.4.cloned.1.call-start = ((), (), s32[]{:S(2)}) async-start(), calls=%async_computation.5 | async-start | bytes 983040 | tf_op jit(solution)/shard_map/reduce_scatter | solution.py:127
  38.0 4.8 %copy-start.7 = (f32[128]{0:T(128)S(1)}, f32[128]{0:T(128)}, u32[]{:S(2)}) copy-start(f32[128]{0:T(128)} %param.23) | copy-start | bytes 1540
  109.7 2.8 copy-start.14
  115.8 1.6 copy-start.11
  115.8 23.6 %copy-start.5 = (bf16[128,768]{1,0:T(8,128)(2,1)S(1)}, bf16[128,768]{1,0:T(8,128)(2,1)}, u32[]{:S(2)}) copy-start(bf16[128,768]{1,0:T(8,128)(2,1)} %param.15) | copy-start | bytes 589828
  117.3 32.0 %copy-start.6 = (f32[3072]{0:T(1024)S(1)}, f32[3072]{0:T(1024)}, u32[]{:S(2)}) copy-start(f32[3072]{0:T(1024)} %param.18) | copy-start | bytes 36868
  117.3 76.2 %all-gather.11.cloned.1.call-start = ((), (), s32[]{:S(2)}) async-start(), calls=%async_computation.7 | async-start | bytes 1179648 | tf_op jit(solution)/shard_map/all_gather | solution.py:67
  148.4 0.9 copy-start.3
  152.5 82.5 %all-gather.9.cloned.1.call-start = ((), (), s32[]{:S(2)}) async-start(), calls=%async_computation.6 | async-start | bytes 1179648 | tf_op jit(solution)/shard_map/all_gather | solution.py:66
  159.3 100.7 %reduce-scatter.8.cloned.1.call-start = ((), (), s32[]{:S(2)}) async-start(), calls=%async_computation.9 | async-start | bytes 983040 | tf_op jit(solution)/shard_map/reduce_scatter | solution.py:136
  163.6 122.2 %reduce-scatter.6.cloned.1.call-start = ((), (), s32[]{:S(2)}) async-start(), calls=%async_computation.8 | async-start | bytes 983040 | tf_op jit(solution)/shard_map/reduce_scatter | solution.py:127
  163.7 71.4 %copy-start.9 = (s32[2,1]{0,1:T(1,128)S(1)}, s32[2,1]{0,1:T(1,128)}, u32[]{:S(2)}) copy-start(s32[2,1]{0,1:T(1,128)} %copy-done.8) | copy-start | bytes 28
  235.1 2.1 copy-start.13
  240.4 45.4 %copy-start.4 = (bf16[128,768]{1,0:T(8,128)(2,1)S(1)}, bf16[128,768]{1,0:T(8,128)(2,1)}, u32[]{:S(2)}) copy-start(bf16[128,768]{1,0:T(8,128)(2,1)} %reduce-scatter.4.cloned.1.call-done) | copy-start | bytes 589828
  240.4 86.6 %copy-start.15 = (s32[2]{0:T(128)S(1)}, s32[2]{0:T(128)}, u32[]{:S(2)}) copy-start(s32[2]{0:T(128)} %param.16) | copy-start | bytes 28
Sparse Core Ops, SparseCore 0:
  26.8 41.1 all-gather.6
  70.7 38.9 all-gather.4
  117.4 21.9 reduce-scatter.3
  152.6 40.8 all-gather.10
  196.0 38.9 all-gather.8
  238.0 21.9 reduce-scatter.7
  262.5 23.2 reduce-scatter.5
where the time goes:
time: 337 us; the launch traced here: 336 us
  waiting for transfers between devices  198 us (59%)
  blocking collectives  57.7 us (17%)
  matrix products  33.4 us (10%)
  between operations  18.7 us (6%)
  other arithmetic  16.8 us (5%)
  local copies, waits for them, and re-layouts  11 us (3%)
    all_gather x2, waiting for transfers between devices, teacher(): key_block = lax.all_gather(key_rows, 'seq', axis=0, tiled=True)  83.3 us
    all_gather x2, waiting for transfers between devices, teacher(): value_block = lax.all_gather(value_rows, 'seq', axis=0, tiled=True)  49 us
    reduce_scatter x2, waiting for transfers between devices, on_device(): lax.psum_scatter(partial_value.astype(jnp.bfloat16), 'tp', scatter_dimens...  47.8 us
    psum x1, blocking collectives, on_device(): image_sum = lax.psum(image_part, ('seq', 'tp'))  39.3 us
    reduce_scatter x1, waiting for transfers between devices, on_device(): lax.psum_scatter(student_terms.astype(jnp.bfloat16), 'tp', scatter_dimens...  18.1 us
    all_gather x1, blocking collectives, on_device(): whole_rows = lax.all_gather(latents, 'tp', axis=1, tiled=True)  10.4 us
    all_gather x1, blocking collectives, on_device(): whole_rows = lax.all_gather(state_shard, 'tp', axis=1, tiled=True)  8.03 us
    dot_general x2, matrix products, teacher(): jnp.dot(hidden, k_weight, preferred_element_type=jnp.float32)  7.02 us
  transfers between devices with their start and end apart: 7, of which 7 were waited for; matrix products, arithmetic and copies ran while one was open for 11% of the time, Pallas kernels for 0%

commit v1 on v0

--- a/solution.py
+++ b/solution.py
@@ -145,7 +145,7 @@
         student32 * student32, axis=1
     )
     image_part = jnp.sum(one_hot * per_token[:, None], axis=0)
-    image_sum = lax.psum(image_part, ("seq", "tp"))
+    image_sum = lax.psum(lax.psum(image_part, axis_name="tp"), axis_name="seq")
     loss = jnp.mean(image_sum / (lengths.astype(jnp.float32) * mod_scale.shape[0]))
     return (target, student_velocity, loss)
 

time: 337 us -> 325 us (0.964)
  blocking collectives: 57.7 us -> 45.7 us
    psum x1 -> x2, blocking collectives: 39.3 us -> 27.3 us  [on_device(): image_sum = lax.psum(lax.psum(image_part, axis_name='tp'), axis_name='seq')]
where the time goes in v1:
time: 325 us; the launch traced here: 324 us
  waiting for transfers between devices  198 us (61%)
  blocking collectives  45.7 us (14%)
  matrix products  33.4 us (10%)
  between operations  18.7 us (6%)
  other arithmetic  16.8 us (5%)
  local copies, waits for them, and re-layouts  11 us (3%)
    all_gather x2, waiting for transfers between devices, teacher(): key_block = lax.all_gather(key_rows, 'seq', axis=0, tiled=True)  83.3 us
    all_gather x2, waiting for transfers between devices, teacher(): value_block = lax.all_gather(value_rows, 'seq', axis=0, tiled=True)  49 us
    reduce_scatter x2, waiting for transfers between devices, on_device(): lax.psum_scatter(partial_value.astype(jnp.bfloat16), 'tp', scatter_dimens...  47.8 us
    psum x2, blocking collectives, on_device(): image_sum = lax.psum(lax.psum(image_part, axis_name='tp'), axis_name='seq')  27.3 us
    reduce_scatter x1, waiting for transfers between devices, on_device(): lax.psum_scatter(student_terms.astype(jnp.bfloat16), 'tp', scatter_dimens...  18.1 us
    all_gather x1, blocking collectives, on_device(): whole_rows = lax.all_gather(latents, 'tp', axis=1, tiled=True)  10.4 us
    all_gather x1, blocking collectives, on_device(): whole_rows = lax.all_gather(state_shard, 'tp', axis=1, tiled=True)  8.03 us
    dot_general x2, matrix products, teacher(): jnp.dot(hidden, k_weight, preferred_element_type=jnp.float32)  7.02 us
  transfers between devices with their start and end apart: 7, of which 7 were waited for; matrix products, arithmetic and copies ran while one was open for 11% of the time, Pallas kernels for 0%

profile of v1, /device:TPU:0, one launch (start us, length us, event | category | flops | bytes accessed | tf_op | source)
XLA Modules:
  0.0 324.3 jit_solution(381760950746596017)
XLA Ops:
  7.2 0.8 convert_multiply_fusion.6
  8.1 10.4 %all_gather.18 = bf16[128,3072]{1,0:T(8,128)(2,1)S(1)} all-gather(bf16[128,768]{1,0:T(8,128)(2,1)} %param.15), channel_id=1, replica_groups=mesh['seq'=8,'tp'=4] {'tp'}, dimensions={1}, use_global_device_ids=true | all-gather | bytes 983040 | tf_op jit(solution)/shard_map/all_gather | solution.py:105
  18.5 0.9 copy-done.2
  19.3 0.2 fusion.36
  19.6 0.8 reduce-window.4
  20.4 0.1 fusion.58
  20.5 0.1 select_reduce_fusion.1
  20.6 0.6 copy-done.10
  21.2 1.5 fusion.38
  22.7 0.9 copy-done.1
  23.6 3.1 convolution_convert_fusion.4
  26.8 3.4 %fusion.70 = (f32[128,512]{1,0:T(8,128)}, f32[128,512]{1,0:T(8,128)S(1)}) fusion(bf16[128,3072]{1,0:T(8,128)(2,1)} %copy-done.1, bf16[3072,512]{1,0:T(8,128)(2,1)} %param.20), kind=kOutput, calls=%fused_computation.115 | convolution fusion | flops 402718720 | bytes 4456448 | tf_op jit(solution)/shard_map/dot_general | solution.py:31
  30.2 1.8 mul.218
  32.0 1.2 reduce_sum.175
  33.2 0.2 mul.219
  33.4 0.7 fusion.52
  34.2 0.7 fusion.69
  34.8 0.6 fusion.60
  38.0 2.7 fusion.72
  40.7 0.8 reshape.212
  41.5 1.2 multiply_reduce_fusion.1
  42.8 0.1 fusion.56
  42.9 25.1 %all-gather.7.cloned.1.call-done = bf16[1024,512]{1,0:T(8,128)(2,1)} async-done(((bf16[128,512]{1,0:T(8,128)(2,1)}), bf16[1024,512]{1,0:T(8,128)(2,1)}) %all-gather.7.cloned.1.call-update) | async-done | bytes 1048592 | tf_op jit(solution)/shard_map/all_gather | solution.py:67
  68.0 41.7 %all-gather.5.cloned.1.call-done = bf16[1024,512]{1,0:T(8,128)(2,1)} async-done(((bf16[128,512]{1,0:T(8,128)(2,1)}), bf16[1024,512]{1,0:T(8,128)(2,1)}) %all-gather.5.cloned.1.call-update) | async-done | bytes 1048592 | tf_op jit(solution)/shard_map/all_gather | solution.py:66
  109.7 6.0 %conditional.2 = (f32[128,4]{0,1:T(4,128)S(1)}, f32[128,4,128]{0,2,1:T(8,128)S(1)}) conditional(s32[]{:T(128)} %convert_element_type.124, () %tuple.24, (s32[128]{0:T(128)S(1)}, s32[2]{0:T(128)}, bf16[1024,512]{1,0:T(8,128)(2,1)}, bf16[128,4,128]{2,0,1:T(8,128)(2,1)S(1)}, bf16[1024,512]{1,0:T(8,128)(2,1)}) %tuple.59), branch_computations={%region_8.9_spmd, %region_9.13_spmd} | conditional | flops 275386880 | bytes 14045748 | solution.py:72
  109.7 0.8 fusion.14
  110.5 0.2 broadcast_compare_fusion
  110.7 1.7 fusion
  112.5 1.6 convolution_bitcast_fusion
  114.1 0.5 fusion.2
  114.6 1.1 copy.83
  115.8 1.5 convolution_convert_fusion.1
  117.4 22.0 %reduce-scatter.4.cloned.1.call-done = bf16[128,768]{1,0:T(8,128)(2,1)} async-done(((bf16[128,3072]{1,0:T(8,128)(2,1)}), bf16[128,768]{1,0:T(8,128)(2,1)}) %reduce-scatter.4.cloned.1.call-update) | async-done | bytes 196624 | tf_op jit(solution)/shard_map/reduce_scatter | solution.py:127
  139.4 1.0 fusion.43
  140.4 8.0 %all_gather.21 = bf16[128,3072]{1,0:T(8,128)(2,1)S(1)} all-gather(bf16[128,768]{1,0:T(8,128)(2,1)S(1)} %fusion.43), channel_id=1, replica_groups=mesh['seq'=8,'tp'=4] {'tp'}, dimensions={1}, use_global_device_ids=true | all-gather | bytes 983040 | tf_op jit(solution)/shard_map/all_gather | solution.py:111
  148.4 0.2 fusion.39
  148.7 0.6 copy-done.3
  149.3 3.2 convolution_convert_fusion.3
  152.6 3.6 %fusion.71 = (f32[128,512]{1,0:T(8,128)}, f32[128,512]{1,0:T(8,128)}) fusion(bf16[3072,512]{1,0:T(8,128)(2,1)} %param.20, bf16[128,3072]{1,0:T(8,128)(2,1)} %copy-done.3, f32[128]{0:T(128)S(1)} %broadcast_add_fusion, f32[128]{0:T(128)S(1)} %add_rsqrt_fusion.4, f32[3072]{0:T(1024)S(1)} %copy-done.6), kind=kOutput, calls=%fused_computation.116 | convolution fusion | flops 405078016 | bytes 4469760 | tf_op jit(solution)/shard_map/dot_general | solution.py:31
  156.2 1.0 mul.240
  157.2 0.2 reduce_sum.178
  157.4 0.2 mul.241
  157.6 1.6 fusion.50
  159.4 4.2 %convolution_convert_fusion.2 = bf16[128,3072]{1,0:T(8,128)(2,1)} fusion(bf16[768,3072]{1,0:T(8,128)(2,1)} %param.25, bf16[128,3072]{1,0:T(8,128)(2,1)} %copy-done.1, s32[]{:T(128)S(6)} %select_n.16), kind=kOutput, calls=%fused_computation.48 | convolution fusion | flops 604372992 | bytes 5701636 | tf_op jit(solution)/shard_map/dot_general | solution.py:135
  163.7 3.5 %fusion.64 = f32[128,512]{1,0:T(8,128)} fusion(bf16[3072,512]{1,0:T(8,128)(2,1)} %param.19, bf16[128,3072]{1,0:T(8,128)(2,1)} %copy-done.3, f32[128]{0:T(128)S(1)} %broadcast_add_fusion, f32[128]{0:T(128)S(1)} %add_rsqrt_fusion.4, f32[3072]{0:T(1024)S(1)} %copy-done.6), kind=kOutput, calls=%fused_computation.112 | convolution fusion | flops 405012480 | bytes 4207616 | tf_op jit(solution)/shard_map/dot_general | solution.py:30
  167.2 1.0 reshape.214
  168.2 0.2 multiply_reduce_fusion
  168.5 1.1 fusion.54
  169.6 23.9 %all-gather.11.cloned.1.call-done = bf16[1024,512]{1,0:T(8,128)(2,1)} async-done(((bf16[128,512]{1,0:T(8,128)(2,1)}), bf16[1024,512]{1,0:T(8,128)(2,1)}) %all-gather.11.cloned.1.call-update) | async-done | bytes 1048592 | tf_op jit(solution)/shard_map/all_gather | solution.py:67
  193.5 41.6 %all-gather.9.cloned.1.call-done = bf16[1024,512]{1,0:T(8,128)(2,1)} async-done(((bf16[128,512]{1,0:T(8,128)(2,1)}), bf16[1024,512]{1,0:T(8,128)(2,1)}) %all-gather.9.cloned.1.call-update) | async-done | bytes 1048592 | tf_op jit(solution)/shard_map/all_gather | solution.py:66
  235.1 5.3 %conditional.3 = (f32[128,4]{0,1:T(4,128)S(1)}, f32[128,4,128]{0,2,1:T(8,128)S(1)}) conditional(s32[]{:T(128)} %convert_element_type.124, () %tuple.26, (s32[128]{0:T(128)S(1)}, s32[2]{0:T(128)S(1)}, bf16[1024,512]{1,0:T(8,128)(2,1)}, bf16[128,4,128]{2,0,1:T(8,128)(2,1)S(1)}, bf16[1024,512]{1,0:T(8,128)(2,1)}) %tuple.60), branch_computations={%region_17.18_spmd, %region_18.0_spmd} | conditional | flops 275386880 | bytes 14045748 | solution.py:72
  235.2 0.2 broadcast_compare_fusion.1
  235.4 1.8 fusion.18
  237.2 1.6 convolution_bitcast_fusion.1
  238.8 0.5 fusion.20
  239.3 1.1 copy.85
  240.4 1.5 convolution_convert_fusion
  242.0 18.1 %reduce-scatter.8.cloned.1.call-done = bf16[128,768]{1,0:T(8,128)(2,1)} async-done(((bf16[128,3072]{1,0:T(8,128)(2,1)}), bf16[128,768]{1,0:T(8,128)(2,1)}) %reduce-scatter.8.cloned.1.call-update) | async-done | bytes 196624 | tf_op jit(solution)/shard_map/reduce_scatter | solution.py:136
  260.0 25.8 %reduce-scatter.6.cloned.1.call-done = bf16[128,768]{1,0:T(8,128)(2,1)} async-done(((bf16[128,3072]{1,0:T(8,128)(2,1)}), bf16[128,768]{1,0:T(8,128)(2,1)}) %reduce-scatter.6.cloned.1.call-update) | async-done | bytes 196624 | tf_op jit(solution)/shard_map/reduce_scatter | solution.py:127
  285.8 1.8 fusion.48
  287.6 0.1 select_reduce_fusion
  287.8 5.8 %psum.14 = f32[2]{0:T(128)S(1)} all-reduce(f32[2]{0:T(128)S(1)} %select_reduce_fusion), channel_id=1, replica_groups=mesh['seq'=8,'tp'=4] {'tp'}, use_global_device_ids=true, to_apply=%region_27.28 | all-reduce | flops 2 | bytes 16 | tf_op jit(solution)/shard_map/psum | solution.py:148
  293.5 21.5 %psum.15 = f32[2]{0:T(128)S(1)} all-reduce(f32[2]{0:T(128)S(1)} %psum.14), channel_id=1, replica_groups=mesh['seq'=8,'tp'=4] {'seq'}, use_global_device_ids=true, to_apply=%region_28.29 | all-reduce | flops 2 | bytes 16 | tf_op jit(solution)/shard_map/psum | solution.py:148
  315.0 0.6 fusion.61
  (59 shorter events, 0.8 us)
Async XLA Ops:
  7.2 108.6 %copy-start = (bf16[512,3072]{1,0:T(8,128)(2,1)S(1)}, bf16[512,3072]{1,0:T(8,128)(2,1)}, u32[]{:S(2)}) copy-start(bf16[512,3072]{1,0:T(8,128)(2,1)} %param.22) | copy-start | bytes 9437188
  7.2 60.8 %all-gather.7.cloned.1.call-start = ((), (), s32[]{:S(2)}) async-start(), calls=%async_computation.4 | async-start | bytes 1179648 | tf_op jit(solution)/shard_map/all_gather | solution.py:67
  18.5 0.9 copy-start.2
  20.4 14.4 %copy-start.8 = (s32[2,1]{0,1:T(1,128)}, s32[2,1]{0,1:T(1,128)S(1)}, u32[]{:S(2)}) copy-start(s32[2,1]{0,1:T(1,128)S(1)} %reduce-window.4) | copy-start | bytes 28
  20.6 0.6 copy-start.10
  22.7 0.9 copy-start.1
  26.7 6.4 %copy-start.12 = (f32[128]{0:T(128)S(1)}, f32[128]{0:T(128)}, u32[]{:S(2)}) copy-start(f32[128]{0:T(128)} %param.24) | copy-start | bytes 1540
  26.7 83.0 %all-gather.5.cloned.1.call-start = ((), (), s32[]{:S(2)}) async-start(), calls=%async_computation.3 | async-start | bytes 1179648 | tf_op jit(solution)/shard_map/all_gather | solution.py:66
  34.1 105.3 %reduce-scatter.4.cloned.1.call-start = ((), (), s32[]{:S(2)}) async-start(), calls=%async_computation.5 | async-start | bytes 983040 | tf_op jit(solution)/shard_map/reduce_scatter | solution.py:127
  38.0 4.8 %copy-start.7 = (f32[128]{0:T(128)S(1)}, f32[128]{0:T(128)}, u32[]{:S(2)}) copy-start(f32[128]{0:T(128)} %param.23) | copy-start | bytes 1540
  109.7 2.8 copy-start.14
  115.8 1.6 copy-start.11
  115.8 23.6 %copy-start.5 = (bf16[128,768]{1,0:T(8,128)(2,1)S(1)}, bf16[128,768]{1,0:T(8,128)(2,1)}, u32[]{:S(2)}) copy-start(bf16[128,768]{1,0:T(8,128)(2,1)} %param.15) | copy-start | bytes 589828
  117.3 32.0 %copy-start.6 = (f32[3072]{0:T(1024)S(1)}, f32[3072]{0:T(1024)}, u32[]{:S(2)}) copy-start(f32[3072]{0:T(1024)} %param.18) | copy-start | bytes 36868
  117.3 76.2 %all-gather.11.cloned.1.call-start = ((), (), s32[]{:S(2)}) async-start(), calls=%async_computation.7 | async-start | bytes 1179648 | tf_op jit(solution)/shard_map/all_gather | solution.py:67
  148.4 0.9 copy-start.3
  152.5 82.5 %all-gather.9.cloned.1.call-start = ((), (), s32[]{:S(2)}) async-start(), calls=%async_computation.6 | async-start | bytes 1179648 | tf_op jit(solution)/shard_map/all_gather | solution.py:66
  159.3 100.7 %reduce-scatter.8.cloned.1.call-start = ((), (), s32[]{:S(2)}) async-start(), calls=%async_computation.9 | async-start | bytes 983040 | tf_op jit(solution)/shard_map/reduce_scatter | solution.py:136
  163.6 122.2 %reduce-scatter.6.cloned.1.call-start = ((), (), s32[]{:S(2)}) async-start(), calls=%async_computation.8 | async-start | bytes 983040 | tf_op jit(solution)/shard_map/reduce_scatter | solution.py:127
  163.7 71.4 %copy-start.9 = (s32[2,1]{0,1:T(1,128)S(1)}, s32[2,1]{0,1:T(1,128)}, u32[]{:S(2)}) copy-start(s32[2,1]{0,1:T(1,128)} %copy-done.8) | copy-start | bytes 28
  235.1 2.1 copy-start.13
  240.4 45.4 %copy-start.4 = (bf16[128,768]{1,0:T(8,128)(2,1)S(1)}, bf16[128,768]{1,0:T(8,128)(2,1)}, u32[]{:S(2)}) copy-start(bf16[128,768]{1,0:T(8,128)(2,1)} %reduce-scatter.4.cloned.1.call-done) | copy-start | bytes 589828
  240.4 74.6 %copy-start.15 = (s32[2]{0:T(128)S(1)}, s32[2]{0:T(128)}, u32[]{:S(2)}) copy-start(s32[2]{0:T(128)} %param.16) | copy-start | bytes 28
Sparse Core Ops, SparseCore 0:
  26.8 41.1 all-gather.6
  70.7 38.9 all-gather.4
  117.4 21.9 reduce-scatter.3
  152.6 40.8 all-gather.10
  196.0 38.9 all-gather.8
  238.0 21.9 reduce-scatter.7
  262.5 23.2 reduce-scatter.5
